TPU v7x, 32 devices: a whole 2x2x4 slice. The times are simulated.
32 devices in a mesh: group: 4 (over y, core), peer: 8 (over z, x).
Axes of the slice: x: 2, y: 2, z: 4, core: 2. Of those that a mesh axis runs over, the one named last changes fastest.
Arguments:
- states: float32 [41, 1048576], P(None, ('group', 'peer')), may hold values from -6 to 6
- block_part: int32 [8192], P(('group', 'peer')), may hold values from 0 to 31, as said below
- tile_perm: int32 [8192, 128], P(('group', 'peer')), may hold values from 0 to 127, each once within a row
- half_volt: float32 [40], replicated, may hold values from -4 to 4
- steepness: float32 [40], replicated, may hold values from 0.5 to 4
- gate_rate: float32 [40], replicated, may hold values from 0.1 to 1
- conductance: float32 [40], replicated, may hold values from 0.005 to 0.08
- reversal: float32 [40], replicated, may hold values from -6 to 6
Outputs:
- regrouped: float32 [41, 1048576], P(None, ('group', 'peer'))
Inputs may be any that keep to these rules, and one draw needn't show every extreme that they name: `block_part`: every partition holds exactly 256 blocks. Within each slab of 256 consecutive global blocks no partition holds more than 16 blocks; every slab has exactly 16 blocks of some partition, and every partition has exactly 16 blocks in some slab.
All inputs are finite; a program needn't handle non-finite values.
Results may differ from a plain program's by a relative error of at most 0.0001.
Values sent between devices are 32-bit elements; how exact they have to be, the bound alone decides.
No kernel may reach another device: no remote copies, remote signals or barrier semaphores. Data moves between devices by JAX's collectives and lax.ppermute only.
A program may use at most 192 MiB of HBM per device.

v0:
```python
import jax
import jax.numpy as jnp
from jax import lax
from jax.sharding import PartitionSpec as P

time_step = 0.25


def entering(part, axis, combine, identity):
    place = lax.axis_index(axis)
    gathered = lax.all_gather(part, axis)
    state = jnp.zeros_like(part) + jnp.asarray(identity, part.dtype)

    def one(step, state):
        return combine(state, lax.dynamic_index_in_dim(gathered, step, 0, False))

    return lax.fori_loop(0, place, one, state)


def advance(state_rows, half_volt, steepness, gate_rate, conductance, reversal):
    voltage = state_rows[0:1]
    gate_vals = state_rows[1:]
    steady = jax.nn.sigmoid((voltage - half_volt[:, None]) * steepness[:, None])
    damping = jnp.exp(-gate_rate[:, None] * (1.0 + jax.nn.sigmoid(voltage)))
    gate_vals = steady + (gate_vals - steady) * damping
    current = jnp.sum(
        conductance[:, None] * gate_vals * (voltage - reversal[:, None]), axis=0, keepdims=True
    )
    voltage = voltage - time_step * current
    return jnp.concatenate([voltage, gate_vals], axis=0)


def add_counts(earlier, later):
    return earlier + later


def on_device(
    states, block_part, tile_perm, half_volt, steepness, gate_rate, conductance, reversal
):
    devices = lax.axis_size(("group", "peer"))
    local_blocks = block_part.shape[0]
    tile_width = tile_perm.shape[1]
    width = states.shape[0]
    capacity = 2 * local_blocks // devices
    partitions = jnp.arange(devices, dtype=jnp.int32)
    onehot = (block_part[:, None] == partitions[None, :]).astype(jnp.int32)
    counts = jnp.sum(onehot, axis=0, dtype=jnp.int32)
    earlier = entering(counts, ("group", "peer"), add_counts, jnp.zeros_like(counts))
    rank_in = jnp.sum(
        (jnp.cumsum(onehot, axis=0, dtype=jnp.int32) - onehot) * onehot, axis=1, dtype=jnp.int32
    )
    local_index = jnp.sum(onehot * earlier[None, :], axis=1, dtype=jnp.int32) + rank_in
    slot_index = block_part * capacity + rank_in
    requests = jnp.full((devices * capacity,), -1, jnp.int32).at[slot_index].set(local_index)
    requests = requests.reshape(devices, capacity)
    advanced = advance(states, half_volt, steepness, gate_rate, conductance, reversal)
    advanced = advanced.reshape(width, local_blocks, tile_width)
    wanted = lax.all_to_all(requests, ("group", "peer"), split_axis=0, concat_axis=0, tiled=True)
    picked = jnp.maximum(wanted, 0).reshape(-1)
    served = jnp.take(advanced, picked, axis=1)
    arrived = lax.all_to_all(
        served.reshape(width, wanted.shape[0], wanted.shape[1], tile_width),
        ("group", "peer"),
        split_axis=1,
        concat_axis=1,
        tiled=True,
    )
    flat_cols = (slot_index[:, None] * tile_width + tile_perm).reshape(-1)
    return jnp.take(arrived.reshape(width, devices * capacity * tile_width), flat_cols, axis=1)


def solution(mesh):
    return jax.shard_map(
        on_device,
        mesh=mesh,
        in_specs=(
            P(None, ("group", "peer")),
            P(("group", "peer")),
            P(("group", "peer"), None),
            P(),
            P(),
            P(),
            P(),
            P(),
        ),
        out_specs=P(None, ("group", "peer")),
        check_vma=False,
    )
```

profile of v0, /device:TPU:25, one launch (start us, length us, event | category | flops | bytes accessed | tf_op | source)
XLA Modules:
  0.0 510.8 jit_solution(10718963295124107990)
XLA Ops:
  0.0 0.8 convert_reduce_fusion
  0.8 0.2 dynamic-update-slice
  1.0 38.3 %all-reduce = s32[1024]{0:T(1024)S(1)} all-reduce(s32[1024]{0:T(1024)S(1)} %dynamic-update-slice), channel_id=2, replica_groups=mesh['group'=4,'peer'=8] {'group','peer'}, use_global_device_ids=true, to_apply=%add | all-reduce | flops 1024 | bytes 8192
  39.4 0.5 while.10
  39.9 0.7 fusion.2
  40.6 0.6 reduce-window.6
  41.2 0.2 slice_reduce_fusion
  41.4 0.8 select_reduce_fusion
  42.2 0.7 broadcast_multiply_fusion.1
  42.9 1.4 scatter_custom_fusion
  44.3 0.7 all_to_all.9
  45.0 7.2 %all-to-all-start = ((s32[32,1,16]{2,1,0:T(1,128)}), s32[32,1,16]{2,1,0:T(1,128)S(1)}, u32[]{:S(2)}, u32[]{:S(2)}) async-start(s32[32,1,16]{2,1,0:T(1,128)} %bitcast.4), calls=%async_computation | async-start | bytes 32768 | tf_op jit(solution)/shard_map/all_to_all | solution.py:58
  52.1 0.7 neg.11
  52.8 1.5 divide_add_fusion
  54.3 6.4 %multiply_reduce_fusion = (f32[32768]{0:T(1024)S(1)}, f32[40,32768]{1,0:T(8,128)S(1)}) fusion(f32[40]{0:T(128)} %param.17, f32[32768]{0:T(1024)S(1)} %bitcast.45, f32[40]{0:T(128)} %param.16, f32[32768]{0:T(1024)S(1)} %bitcast.44, f32[40]{0:T(128)S(1)} %neg.11, f32[41,32768]{1,0:T(8,128)} %param.10, f32[40]{0:T(128)} %param.14, f32[40]{0:T(128)} %param.13), kind=kLoop, calls=%fused_computation.7 | loop fusion | flops 17006592 | bytes 10879776 | tf_op jit(solution)/shard_map/reduce_sum | solution.py:26
  60.7 1.3 slice_subtract_fusion
  62.1 0.5 pad_maximum_fusion
  62.6 1.1 copy.34
  63.7 0.6 slice.21
  64.2 5.9 %copy.29 = f32[41,256,128]{2,0,1:T(8,128)} copy(f32[41,256,128]{2,1,0:T(8,128)S(1)} %slice.21) | data formatting | bytes 10747904 | tf_op jit(solution)/shard_map/reshape | solution.py:57
  70.2 0.1 copy.27
  70.4 0.1 reshape.119
  70.5 8.7 %gather_fusion = f32[512,41,128]{2,1,0:T(8,128)} fusion(f32[41,256,128]{2,0,1:T(8,128)} %copy.29, s32[1024]{0:T(1024)S(1)} %pad_clamp_fusion), kind=kCustom, calls=%fused_computation | custom fusion | bytes 21497856 | tf_op jit(solution)/shard_map/jit(_take)/gather | solution.py:60
  79.2 14.1 %copy_select_fusion = f32[41,32,16,128]{3,2,0,1:T(8,128)} fusion(f32[41,32,16,128]{3,0,2,1:T(8,128)} %bitcast.41, pred[32,16]{1,0:T(8,128)(4,1)S(1)} %copy.27), kind=kLoop, calls=%fused_computation.5 | loop fusion | flops 2686976 | bytes 21496320 | tf_op jit(solution)/shard_map/jit(_take)/select_n | solution.py:60
  93.3 5.9 %all-to-all-start.1 = ((f32[41,32,16,128]{3,2,0,1:T(8,128)}), f32[41,32,16,128]{3,2,0,1:T(8,128)}, u32[]{:S(2)}, u32[]{:S(2)}) async-start(f32[41,32,16,128]{3,2,0,1:T(8,128)} %copy_select_fusion), calls=%async_computation.1 | async-start | bytes 21495808 | tf_op jit(solution)/shard_map/all_to_all | solution.py:61
  99.2 0.1 compare_and_fusion
  99.3 0.1 compare_select_fusion
  99.5 240.6 %all-to-all-done.1 = f32[41,32,16,128]{3,2,0,1:T(8,128)} async-done(((f32[41,32,16,128]{3,2,0,1:T(8,128)}), f32[41,32,16,128]{3,2,0,1:T(8,128)}, u32[]{:S(2)}, u32[]{:S(2)}) %all-to-all-start.1) | async-done | bytes 10747936 | tf_op jit(solution)/shard_map/all_to_all | solution.py:61
  340.0 20.7 %copy.31 = f32[41,32,16,128]{0,3,2,1:T(8,128)} copy(f32[41,32,16,128]{3,2,0,1:T(8,128)} %all-to-all-done.1) | data formatting | bytes 21495808 | tf_op jit(solution)/shard_map/all_to_all | solution.py:61
  360.8 118.8 %gather_fusion.1 = f32[32768,41]{1,0:T(8,128)} fusion(f32[41,65536]{0,1:T(8,128)} %bitcast.40, s32[32768]{0:T(1024)S(1)} %broadcast_clamp_fusion), kind=kCustom, calls=%fused_computation.1 | custom fusion | bytes 10878976 | tf_op jit(solution)/shard_map/jit(_take)/gather | solution.py:69
  479.6 19.1 %select_bitcast_fusion = f32[41,32768]{0,1:T(8,128)} fusion(f32[32768,41]{1,0:T(8,128)} %gather_fusion.1, pred[32768]{0:T(1024)(128)(4,1)S(1)} %get-tuple-element.39), kind=kLoop, calls=%fused_computation.4 | loop fusion | flops 1343488 | bytes 10780672 | tf_op jit(solution)/shard_map/jit(_take)/select_n | solution.py:69
  498.7 12.1 %copy.32 = f32[41,32768]{1,0:T(8,128)} copy(f32[41,32768]{0,1:T(8,128)} %select_bitcast_fusion) | data formatting | bytes 10747904 | tf_op jit(solution)/shard_map/jit(_take)/select_n | solution.py:69
  (29 shorter events, 0.5 us)
Async XLA Ops:
  45.0 25.2 %all-to-all-start = ((s32[32,1,16]{2,1,0:T(1,128)}), s32[32,1,16]{2,1,0:T(1,128)S(1)}, u32[]{:S(2)}, u32[]{:S(2)}) async-start(s32[32,1,16]{2,1,0:T(1,128)} %bitcast.4), calls=%async_computation | async-start | bytes 32768 | tf_op jit(solution)/shard_map/all_to_all | solution.py:58
  93.3 5.9 %copy-start = (s32[256,128]{1,0:T(8,128)S(1)}, s32[256,128]{1,0:T(8,128)}, u32[]{:S(2)}) copy-start(s32[256,128]{1,0:T(8,128)} %param.12) | copy-start | bytes 393220
  93.3 246.8 %all-to-all-start.1 = ((f32[41,32,16,128]{3,2,0,1:T(8,128)}), f32[41,32,16,128]{3,2,0,1:T(8,128)}, u32[]{:S(2)}, u32[]{:S(2)}) async-start(f32[41,32,16,128]{3,2,0,1:T(8,128)} %copy_select_fusion), calls=%async_computation.1 | async-start | bytes 21495808 | tf_op jit(solution)/shard_map/all_to_all | solution.py:61
where the time goes:
time: 512 us; the launch traced here: 511 us
  waiting for transfers between devices  241 us (47%)
  local copies, waits for them, and re-layouts  171 us (33%)
  other arithmetic  47.6 us (9%)
  blocking collectives  38.3 us (7%)
  starting transfers between devices  13 us (3%)
    all_to_all x1, waiting for transfers between devices, on_device(): lax.all_to_all(served.reshape(width, wanted.shape[0], wanted.shape[1], ti...  241 us
    gather x1, local copies, waits for them, and re-layouts, on_device(): jnp.take(arrived.reshape(width, devices * capacity * tile_width), flat_co...  119 us
    unnamed x1, blocking collectives  38.3 us
    all_to_all x1, local copies, waits for them, and re-layouts, on_device(): lax.all_to_all(served.reshape(width, wanted.shape[0], wanted.shape[1], ti...  20.7 us
    select_n x2, other arithmetic, on_device(): jnp.take(arrived.reshape(width, devices * capacity * tile_width), flat_co...  19.2 us
    select_n x1, other arithmetic, on_device(): served = jnp.take(advanced, picked, axis=1)  14.1 us
    select_n x1, local copies, waits for them, and re-layouts, on_device(): jnp.take(arrived.reshape(width, devices * capacity * tile_width), flat_co...  12.1 us
  transfers between devices with their start and end apart: 2, of which 1 were waited for; matrix products, arithmetic and copies ran while one was open for 4% of the time, Pallas kernels for 0%

commit v1 on v0

--- a/solution.py
+++ b/solution.py
@@ -58,12 +58,20 @@
     wanted = lax.all_to_all(requests, ("group", "peer"), split_axis=0, concat_axis=0, tiled=True)
     picked = jnp.maximum(wanted, 0).reshape(-1)
     served = jnp.take(advanced, picked, axis=1)
-    arrived = lax.all_to_all(
-        served.reshape(width, wanted.shape[0], wanted.shape[1], tile_width),
-        ("group", "peer"),
-        split_axis=1,
-        concat_axis=1,
-        tiled=True,
+    arrived = jnp.concatenate(
+        lax.all_to_all(
+            jnp.stack(
+                jnp.split(
+                    served.reshape(width, wanted.shape[0], wanted.shape[1], tile_width),
+                    lax.axis_size(("group", "peer")),
+                    axis=1,
+                )
+            ),
+            ("group", "peer"),
+            0,
+            0,
+        ),
+        axis=1,
     )
     flat_cols = (slot_index[:, None] * tile_width + tile_perm).reshape(-1)
     return jnp.take(arrived.reshape(width, devices * capacity * tile_width), flat_cols, axis=1)

time: 512 us -> 568 us (1.11)
  local copies, waits for them, and re-layouts: 171 us -> 226 us
    unnamed x5 -> x36, local copies, waits for them, and re-layouts: 1.33 us -> 55 us
    all_to_all x1 -> x0, local copies, waits for them, and re-layouts: 20.7 us -> none  [on_device(): lax.all_to_all(served.reshape(width, wanted.shape[0], wanted.shape[1], ti...]
    reshape x0 -> x1, local copies, waits for them, and re-layouts: none -> 20.7 us  [on_device(): jnp.concatenate(lax.all_to_all(jnp.stack(jnp.split(served.reshape(width,...]
  transfers between devices with their start and end apart: 2 -> 2, of which waited for: 1 -> 1; matrix products, arithmetic and copies ran while one was open for 4% -> 3% of each run, Pallas kernels for 0% -> 0%
where the time goes in v1:
time: 568 us; the launch traced here: 566 us
  waiting for transfers between devices  241 us (42%)
  local copies, waits for them, and re-layouts  226 us (40%)
  other arithmetic  47.6 us (8%)
  blocking collectives  38.3 us (7%)
  starting transfers between devices  13 us (2%)
    all_to_all x1, waiting for transfers between devices, on_device(): lax.all_to_all(jnp.stack(jnp.split(served.reshape(width, wanted.shape[0],...  241 us
    gather x1, local copies, waits for them, and re-layouts, on_device(): jnp.take(arrived.reshape(width, devices * capacity * tile_width), flat_co...  119 us
    unnamed x36, local copies, waits for them, and re-layouts  55 us
    unnamed x1, blocking collectives  38.3 us
    reshape x1, local copies, waits for them, and re-layouts, on_device(): jnp.concatenate(lax.all_to_all(jnp.stack(jnp.split(served.reshape(width,...  20.7 us
    select_n x2, other arithmetic, on_device(): jnp.take(arrived.reshape(width, devices * capacity * tile_width), flat_co...  19.2 us
    select_n x1, other arithmetic, on_device(): served = jnp.take(advanced, picked, axis=1)  14.1 us
    select_n x1, local copies, waits for them, and re-layouts, on_device(): jnp.take(arrived.reshape(width, devices * capacity * tile_width), flat_co...  12.1 us
  transfers between devices with their start and end apart: 2, of which 1 were waited for; matrix products, arithmetic and copies ran while one was open for 3% of the time, Pallas kernels for 0%

profile of v1, /device:TPU:25, one launch (start us, length us, event | category | flops | bytes accessed | tf_op | source)
XLA Modules:
  0.0 566.2 jit_solution(7285395196520501991)
XLA Ops:
  1.0 38.3 %all-reduce = s32[1024]{0:T(1024)S(1)} all-reduce(s32[1024]{0:T(1024)S(1)} %dynamic-update-slice), channel_id=2, replica_groups=mesh['group'=4,'peer'=8] {'group','peer'}, use_global_device_ids=true, to_apply=%add | all-reduce | flops 1024 | bytes 8192
  45.0 7.2 %all-to-all-start = ((s32[32,1,16]{2,1,0:T(1,128)}), s32[32,1,16]{2,1,0:T(1,128)S(1)}, u32[]{:S(2)}, u32[]{:S(2)}) async-start(s32[32,1,16]{2,1,0:T(1,128)} %bitcast.4), calls=%async_computation | async-start | bytes 32768 | tf_op jit(solution)/shard_map/all_to_all | solution.py:58
  54.3 6.4 %multiply_reduce_fusion = (f32[32768]{0:T(1024)S(1)}, f32[40,32768]{1,0:T(8,128)S(1)}) fusion(f32[40]{0:T(128)} %param.17, f32[32768]{0:T(1024)S(1)} %bitcast.236, f32[40]{0:T(128)} %param.16, f32[32768]{0:T(1024)S(1)} %bitcast.235, f32[40]{0:T(128)S(1)} %neg.11, f32[41,32768]{1,0:T(8,128)} %param.10, f32[40]{0:T(128)} %param.14, f32[40]{0:T(128)} %param.13), kind=kLoop, calls=%fused_computation.7 | loop fusion | flops 17006592 | bytes 10879776 | tf_op jit(solution)/shard_map/reduce_sum | solution.py:26
  64.2 5.9 %copy.91 = f32[41,256,128]{2,0,1:T(8,128)} copy(f32[41,256,128]{2,1,0:T(8,128)S(1)} %slice.21) | data formatting | bytes 10747904 | tf_op jit(solution)/shard_map/reshape | solution.py:57
  70.5 8.7 %gather_fusion = f32[512,41,128]{2,1,0:T(8,128)} fusion(f32[41,256,128]{2,0,1:T(8,128)} %copy.91, s32[1024]{0:T(1024)S(1)} %pad_clamp_fusion), kind=kCustom, calls=%fused_computation | custom fusion | bytes 21497856 | tf_op jit(solution)/shard_map/jit(_take)/gather | solution.py:60
  79.2 14.1 %copy_select_fusion = f32[41,32,16,128]{3,2,0,1:T(8,128)} fusion(f32[41,32,16,128]{3,0,2,1:T(8,128)} %bitcast.232, pred[32,16]{1,0:T(8,128)(4,1)S(1)} %copy.89), kind=kLoop, calls=%fused_computation.5 | loop fusion | flops 2686976 | bytes 21496320 | tf_op jit(solution)/shard_map/jit(_take)/select_n | solution.py:60
  95.0 1.7 fusion.30
  98.4 1.7 fusion.28
  100.2 1.7 fusion.27
  103.6 1.7 fusion.25
  108.8 1.8 fusion.22
  115.7 1.7 fusion.18
  117.5 1.7 fusion.17
  119.2 1.7 fusion.16
  120.9 1.7 fusion.15
  122.7 1.7 fusion.14
  126.1 1.7 fusion.12
  129.6 1.7 fusion.10
  134.8 1.7 fusion.7
  136.5 1.7 fusion.6
  138.2 1.7 fusion.5
  140.0 1.8 fusion.4
  141.7 1.7 fusion.3
  143.5 1.7 fusion.2
  145.2 1.7 fusion.1
  146.9 1.8 fusion
  148.7 5.9 %all-to-all-start.1 = ((f32[32,41,1,16,128]{4,3,2,1,0:T(8,128)}), f32[32,41,1,16,128]{4,3,2,1,0:T(8,128)}, u32[]{:S(2)}, u32[]{:S(2)}) async-start(f32[32,41,1,16,128]{4,3,2,1,0:T(8,128)} %fusion), calls=%async_computation.1 | async-start | bytes 21495808 | tf_op jit(solution)/shard_map/all_to_all | solution.py:62
  154.9 240.6 %all-to-all-done.1 = f32[32,41,1,16,128]{4,3,2,1,0:T(8,128)} async-done(((f32[32,41,1,16,128]{4,3,2,1,0:T(8,128)}), f32[32,41,1,16,128]{4,3,2,1,0:T(8,128)}, u32[]{:S(2)}, u32[]{:S(2)}) %all-to-all-start.1) | async-done | bytes 10747936 | tf_op jit(solution)/shard_map/all_to_all | solution.py:62
  395.5 20.7 %copy.124 = f32[41,32,1,16,128]{0,4,3,1,2:T(8,128)} copy(f32[41,32,1,16,128]{4,3,2,0,1:T(8,128)} %bitcast.74) | data formatting | bytes 21495808 | tf_op jit(solution)/shard_map/reshape | solution.py:61
  416.2 118.8 %gather_fusion.1 = f32[32768,41]{1,0:T(8,128)} fusion(f32[41,65536]{0,1:T(8,128)} %bitcast.231, s32[32768]{0:T(1024)S(1)} %broadcast_clamp_fusion), kind=kCustom, calls=%fused_computation.1 | custom fusion | bytes 10878976 | tf_op jit(solution)/shard_map/jit(_take)/gather | solution.py:77
  535.0 19.1 %select_bitcast_fusion = f32[41,32768]{0,1:T(8,128)} fusion(f32[32768,41]{1,0:T(8,128)} %gather_fusion.1, pred[32768]{0:T(1024)(128)(4,1)S(1)} %get-tuple-element.39), kind=kLoop, calls=%fused_computation.4 | loop fusion | flops 1343488 | bytes 10780672 | tf_op jit(solution)/shard_map/jit(_take)/select_n | solution.py:77
  554.1 12.1 %copy.125 = f32[41,32768]{1,0:T(8,128)} copy(f32[41,32768]{0,1:T(8,128)} %select_bitcast_fusion) | data formatting | bytes 10747904 | tf_op jit(solution)/shard_map/jit(_take)/select_n | solution.py:77
  (61 shorter events, 33.8 us)
Async XLA Ops:
  45.0 25.2 %all-to-all-start = ((s32[32,1,16]{2,1,0:T(1,128)}), s32[32,1,16]{2,1,0:T(1,128)S(1)}, u32[]{:S(2)}, u32[]{:S(2)}) async-start(s32[32,1,16]{2,1,0:T(1,128)} %bitcast.4), calls=%async_computation | async-start | bytes 32768 | tf_op jit(solution)/shard_map/all_to_all | solution.py:58
  148.7 5.9 %copy-start = (s32[256,128]{1,0:T(8,128)S(1)}, s32[256,128]{1,0:T(8,128)}, u32[]{:S(2)}) copy-start(s32[256,128]{1,0:T(8,128)} %param.12) | copy-start | bytes 393220
  148.7 246.8 %all-to-all-start.1 = ((f32[32,41,1,16,128]{4,3,2,1,0:T(8,128)}), f32[32,41,1,16,128]{4,3,2,1,0:T(8,128)}, u32[]{:S(2)}, u32[]{:S(2)}) async-start(f32[32,41,1,16,128]{4,3,2,1,0:T(8,128)} %fusion), calls=%async_computation.1 | async-start | bytes 21495808 | tf_op jit(solution)/shard_map/all_to_all | solution.py:62
